TPU v7x, 32 devices: a whole 2x2x4 slice. The times are simulated.
32 devices in a mesh: data: 32 (over z, y, x, core).
Axes of the slice: x: 2, y: 2, z: 4, core: 2. Of those that a mesh axis runs over, the one named last changes fastest.
Arguments:
- tokens: bfloat16 [262144, 256], P('data')
- out_grad: bfloat16 [262144, 256], P('data')
- w_up: bfloat16 [2, 256, 1024], replicated
- w_down: bfloat16 [2, 1024, 256], replicated
- a_up_old: float32 [2, 256, 256], replicated
- s_up_old: float32 [2, 1024, 1024], replicated
- a_down_old: float32 [2, 1024, 1024], replicated
- s_down_old: float32 [2, 256, 256], replicated
- a_up_inv: float32 [2, 256, 256], replicated
- s_up_inv: float32 [2, 1024, 1024], replicated
- a_down_inv: float32 [2, 1024, 1024], replicated
- s_down_inv: float32 [2, 256, 256], replicated
- factor_decay: float32 [], replicated
Outputs:
- output 1: float32 [2, 256, 1024], replicated
- output 2: float32 [2, 1024, 256], replicated
- output 3: float32 [2, 256, 256], replicated
- output 4: float32 [2, 1024, 1024], replicated
- output 5: float32 [2, 1024, 1024], replicated
- output 6: float32 [2, 256, 256], replicated
All inputs are finite; a program needn't handle non-finite values.
Results may differ from a plain program's by a relative error of at most 0.00171367.
Values are sent between devices in bfloat16 or wider.
A program may use at most 1 GiB of HBM per device.

v0:
```python
import jax
import jax.numpy as jnp
from jax import lax
from jax.sharding import PartitionSpec as P, NamedSharding


def gelu_fn(pre_act):
    return jax.nn.gelu(pre_act, approximate=True)


def cross_sum(left, right):
    return jnp.einsum("ti,tj->ij", left, right, preferred_element_type=jnp.float32)


def stacked_sums(left_list, right_list, batch_total):
    return jnp.stack([cross_sum(left, right) for left, right in zip(left_list, right_list)]) / batch_total


def precise_chain(left, middle, right):
    inner_prod = jnp.einsum("bij,bjk->bik", left, middle, precision=lax.Precision.HIGHEST,
                            preferred_element_type=jnp.float32)
    return jnp.einsum("bij,bjk->bik", inner_prod, right, precision=lax.Precision.HIGHEST,
                      preferred_element_type=jnp.float32)


def forward_backward(tok_rows, grad_rows, w_up, w_down):
    block_count = w_up.shape[0]
    layer_ins = []
    pre_ups = []
    hiddens = []
    layer_in = tok_rows
    for block_idx in range(block_count):
        pre_up = jnp.dot(layer_in, w_up[block_idx], preferred_element_type=jnp.float32).astype(jnp.bfloat16)
        hidden = gelu_fn(pre_up.astype(jnp.float32)).astype(jnp.bfloat16)
        layer_ins.append(layer_in)
        pre_ups.append(pre_up)
        hiddens.append(hidden)
        if block_idx + 1 < block_count:
            layer_in = jnp.dot(hidden, w_down[block_idx], preferred_element_type=jnp.float32).astype(jnp.bfloat16)
    grad_ups = [None] * block_count
    grad_downs = [None] * block_count
    grad_down = grad_rows
    for block_idx in reversed(range(block_count)):
        grad_downs[block_idx] = grad_down
        d_hidden = jnp.einsum("tj,ij->ti", grad_down, w_down[block_idx],
                              preferred_element_type=jnp.float32).astype(jnp.bfloat16)
        gelu_back = jax.vjp(gelu_fn, pre_ups[block_idx].astype(jnp.float32))[1]
        grad_up = gelu_back(d_hidden.astype(jnp.float32))[0].astype(jnp.bfloat16)
        grad_ups[block_idx] = grad_up
        if block_idx > 0:
            grad_down = jnp.einsum("tj,ij->ti", grad_up, w_up[block_idx],
                                   preferred_element_type=jnp.float32).astype(jnp.bfloat16)
    return layer_ins, hiddens, grad_ups, grad_downs


def update_outputs(dw_up, dw_down, fresh_factors, old_factors, inverses, factor_decay):
    new_factors = tuple(factor_decay * old_part + (1.0 - factor_decay) * new_part
                        for old_part, new_part in zip(old_factors, fresh_factors))
    precond_up = precise_chain(inverses[0], dw_up, inverses[1])
    precond_down = precise_chain(inverses[2], dw_down, inverses[3])
    return (precond_up, precond_down) + new_factors


def solution(mesh):
    axis_size = mesh.shape["data"]

    def local_step(tok_rows, grad_rows, w_up, w_down, a_up_old, s_up_old, a_down_old, s_down_old,
                   a_up_inv, s_up_inv, a_down_inv, s_down_inv, factor_decay):
        batch_total = tok_rows.shape[0] * axis_size
        layer_ins, hiddens, grad_ups, grad_downs = forward_backward(tok_rows, grad_rows, w_up, w_down)
        local_parts = (stacked_sums(layer_ins, grad_ups, batch_total),
                       stacked_sums(hiddens, grad_downs, batch_total),
                       stacked_sums(layer_ins, layer_ins, batch_total),
                       stacked_sums(grad_ups, grad_ups, batch_total),
                       stacked_sums(hiddens, hiddens, batch_total),
                       stacked_sums(grad_downs, grad_downs, batch_total))
        totals = [lax.psum(part, "data") for part in local_parts]
        return update_outputs(totals[0], totals[1], tuple(totals[2:]),
                              (a_up_old, s_up_old, a_down_old, s_down_old),
                              (a_up_inv, s_up_inv, a_down_inv, s_down_inv), factor_decay)

    batch_spec = P("data", None)
    replicated = P()
    return jax.shard_map(local_step, mesh=mesh, in_specs=(batch_spec, batch_spec) + (replicated,) * 11,
                         out_specs=(replicated,) * 6, check_vma=False)
```

profile of v0, /device:TPU:0, one launch (start us, length us, event | category | flops | bytes accessed | tf_op | source)
XLA Modules:
  0.0 708.2 jit_solution(1727309203257835502)
XLA Ops:
  7.2 5.5 convolution_bitcast_fusion.11
  12.7 15.3 %fusion.13 = (bf16[8192,1024]{1,0:T(8,128)(2,1)S(1)}, bf16[8192,1024]{1,0:T(8,128)(2,1)}) fusion(bf16[8192,256]{1,0:T(8,128)(2,1)} %param.13, bf16[2,256,1024]{2,1,0:T(8,128)(2,1)} %param.15), kind=kOutput, calls=%fused_computation.25 | convolution fusion | flops 4387241984 | bytes 38273024 | tf_op jit(solution)/shard_map/dot_general | solution.py:33
  28.0 19.2 %convolution_bitcast_fusion.1 = f32[1,1024,1024]{2,1,0:T(8,128)} fusion(bf16[8192,1024]{1,0:T(8,128)(2,1)S(1)} %get-tuple-element.12), kind=kOutput, calls=%fused_computation.43 | convolution fusion | flops 17179869184 | bytes 20971520 | tf_op jit(solution)/shard_map/ti,tj->ij/dot_general | solution.py:12
  47.2 6.2 convolution_convert_fusion.3
  53.4 2.0 copy-done.2
  55.4 2.0 convolution_bitcast_fusion.10
  57.4 10.3 %convolution_convert_fusion = bf16[8192,1024]{1,0:T(8,128)(2,1)} fusion(bf16[8192,256]{1,0:T(8,128)(2,1)} %copy-done.2, bf16[2,256,1024]{2,1,0:T(8,128)(2,1)S(1)} %copy-done.18), kind=kOutput, calls=%fused_computation.34 | convolution fusion | flops 4303355904 | bytes 21495808 | tf_op jit(solution)/shard_map/dot_general | solution.py:33
  67.8 5.6 convolution_bitcast_fusion.8
  73.4 17.5 %convolution_bitcast_fusion.5 = f32[1,1024,256]{2,1,0:T(8,128)} fusion(bf16[8192,256]{1,0:T(8,128)(2,1)} %param.14, bf16[8192,1024]{1,0:T(8,128)(2,1)} %convolution_convert_fusion), kind=kOutput, calls=%fused_computation.49 | convolution fusion | flops 4378853376 | bytes 22020096 | tf_op jit(solution)/shard_map/ti,tj->ij/dot_general | solution.py:12
  90.9 43.6 %convolution_bitcast_fusion = f32[1,1024,1024]{2,1,0:T(8,128)} fusion(bf16[8192,1024]{1,0:T(8,128)(2,1)S(1)} %bitcast.80), kind=kOutput, calls=%fused_computation.42 | convolution fusion | flops 17263755264 | bytes 20971520 | tf_op jit(solution)/shard_map/ti,tj->ij/dot_general | solution.py:12
  134.5 26.5 %fusion.4 = bf16[8192,1024]{1,0:T(8,128)(2,1)} fusion(bf16[8192,1024]{1,0:T(8,128)(2,1)S(1)} %bitcast.80, bf16[8192,256]{1,0:T(8,128)(2,1)S(1)} %copy-done.3, bf16[2,1024,256]{2,1,0:T(8,128)(2,1)S(1)} %copy-done.19), kind=kOutput, calls=%fused_computation.16 | convolution fusion | flops 4487905280 | bytes 38273024 | tf_op jit(solution)/shard_map/tj,ij->ti/dot_general | solution.py:45
  160.9 11.7 %convolution_bitcast_fusion.4 = f32[1,256,1024]{1,2,0:T(8,128)S(1)} fusion(bf16[8192,256]{1,0:T(8,128)(2,1)} %copy-done.2, bf16[8192,1024]{1,0:T(8,128)(2,1)} %fusion.4), kind=kOutput, calls=%fused_computation.48 | convolution fusion | flops 4294967296 | bytes 22020096 | tf_op jit(solution)/shard_map/ti,tj->ij/dot_general | solution.py:12
  172.6 10.4 %convolution_convert_fusion.2 = bf16[8192,256]{1,0:T(8,128)(2,1)S(1)} fusion(bf16[8192,1024]{1,0:T(8,128)(2,1)} %fusion.4, bf16[2,256,1024]{2,1,0:T(8,128)(2,1)S(1)} %copy-done.18), kind=kOutput, calls=%fused_computation.36 | convolution fusion | flops 4297064448 | bytes 21495808 | tf_op jit(solution)/shard_map/tj,ij->ti/dot_general | solution.py:51
  183.0 26.1 %convolution_bitcast_fusion.2 = f32[1,1024,1024]{2,1,0:T(8,128)} fusion(bf16[8192,1024]{1,0:T(8,128)(2,1)} %fusion.4), kind=kOutput, calls=%fused_computation.44 | convolution fusion | flops 17179869184 | bytes 20971520 | tf_op jit(solution)/shard_map/ti,tj->ij/dot_general | solution.py:12
  209.1 8.4 %convolution_bitcast_fusion.6 = f32[1,1024,256]{2,1,0:T(8,128)S(1)} fusion(bf16[8192,1024]{1,0:T(8,128)(2,1)} %copy-done.4, bf16[8192,256]{1,0:T(8,128)(2,1)S(1)} %convolution_convert_fusion.2), kind=kOutput, calls=%fused_computation.50 | convolution fusion | flops 4294967296 | bytes 22020096 | tf_op jit(solution)/shard_map/ti,tj->ij/dot_general | solution.py:12
  217.5 1.3 convolution_bitcast_fusion.9
  218.8 28.4 %fusion.7 = bf16[8192,1024]{1,0:T(8,128)(2,1)} fusion(bf16[8192,1024]{1,0:T(8,128)(2,1)} %get-tuple-element.13, bf16[8192,256]{1,0:T(8,128)(2,1)S(1)} %convolution_convert_fusion.2, bf16[2,1024,256]{2,1,0:T(8,128)(2,1)S(1)} %copy-done.20), kind=kOutput, calls=%fused_computation.19 | convolution fusion | flops 4487905280 | bytes 38273024 | tf_op jit(solution)/shard_map/tj,ij->ti/dot_general | solution.py:45
  247.3 8.3 %convolution_bitcast_fusion.7 = f32[1,256,1024]{1,2,0:T(8,128)S(1)} fusion(bf16[8192,1024]{1,0:T(8,128)(2,1)} %fusion.7, bf16[8192,256]{1,0:T(8,128)(2,1)S(1)} %copy-done.1), kind=kOutput, calls=%fused_computation.51 | convolution fusion | flops 4294967296 | bytes 22020096 | tf_op jit(solution)/shard_map/ti,tj->ij/dot_general | solution.py:12
  255.6 2.2 copy-done.5
  257.8 19.4 %convolution_bitcast_fusion.3 = f32[1,1024,1024]{2,1,0:T(8,128)} fusion(bf16[8192,1024]{1,0:T(8,128)(2,1)S(1)} %copy-done.5), kind=kOutput, calls=%fused_computation.45 | convolution fusion | flops 17179869184 | bytes 20971520 | tf_op jit(solution)/shard_map/ti,tj->ij/dot_general | solution.py:12
  277.2 0.8 maximum_multiply_fusion.4
  278.1 9.4 %maximum_multiply_fusion.1 = f32[2,1024,1024]{2,1,0:T(8,128)} fusion(f32[1,1024,1024]{2,1,0:T(8,128)} %convolution_bitcast_fusion, f32[1,1024,1024]{2,1,0:T(8,128)} %convolution_bitcast_fusion.1), kind=kLoop, calls=%fused_computation.39 | loop fusion | flops 4194304 | bytes 16777216 | tf_op jit(solution)/shard_map/div | solution.py:16
  288.3 1.5 maximum_multiply_fusion.3
  289.7 4.4 maximum_multiply_fusion
  294.1 1.5 maximum_multiply_fusion.2
  296.3 357.7 %all-reduce.3.cloned.1.call-done = (f32[2,256,1024]{1,2,0:T(8,128)}, f32[2,1024,256]{2,1,0:T(8,128)}, f32[2,256,256]{2,1,0:T(8,128)}, f32[2,1024,1024]{2,1,0:T(8...) async-done(((f32[2,256,1024]{1,2,0:T(8,128)}, f32[2,1024,256]{2,1,0:T(8,128)}, f32[2,256,256]{2,1,0:T(8,128)}, f32[2,1024,1024]{2,1,0:T(8,128)}, ...) | async-done | bytes 22020112 | tf_op jit(solution)/shard_map/psum | solution.py:77
  654.1 3.7 fusion.36
  657.8 10.8 %fusion.37 = f32[2,256,1024]{2,1,0:T(8,128)} fusion(f32[2,1024,256]{1,2,0:T(8,128)S(1)} %fusion.36, f32[2,1024,1024]{2,1,0:T(8,128)} %param.22), kind=kOutput, calls=%fused_computation.73 | convolution fusion | flops 6442450944 | bytes 12582912 | tf_op jit(solution)/shard_map/bij,bjk->bik/dot_general | solution.py:22
  668.6 9.2 %fusion.38 = f32[2,256,1024]{1,2,0:T(8,128)S(1)} fusion(f32[2,1024,256]{2,1,0:T(8,128)S(1)} %copy-done.8, f32[2,1024,1024]{2,1,0:T(8,128)} %param.23), kind=kOutput, calls=%fused_computation.74 | convolution fusion | flops 6442450944 | bytes 12582912 | tf_op jit(solution)/shard_map/bij,bjk->bik/dot_general | solution.py:20
  677.8 3.3 fusion.39
  681.1 1.1 multiply_add_fusion.2
  682.2 18.8 %multiply_add_fusion = (f32[2,1024,1024]{2,1,0:T(8,128)}, f32[2,1024,1024]{2,1,0:T(8,128)}) fusion(f32[2,1024,1024]{2,1,0:T(8,128)} %get-tuple-element.10, f32[2,1024,1024]{2,1,0:T(8,128)} %param.19, f32[]{:T(128)S(6)} %sub.14, f32[]{:T(128)S(6)} %copy.27, f32[2,1024,1024]{2,1,0:T(8,128)} %get-tuple-element.9, f32[2,1024,1024]{2,1,0:T(8,128)} %param.18), kind=kLoop, calls=%fused_computation.40 | loop fusion | flops 12582912 | bytes 50331656 | tf_op jit(solution)/shard_map/add | solution.py:57
  (52 shorter events, 1.0 us)
Async XLA Ops:
  7.2 646.9 %copy-start = (f32[2,256,256]{2,1,0:T(8,128)S(1)}, f32[2,256,256]{2,1,0:T(8,128)}, u32[]{:S(2)}) copy-start(f32[2,256,256]{2,1,0:T(8,128)} %param.21) | copy-start | bytes 1572868
  7.2 646.9 %all-reduce.3.cloned.1.call-start = ((), (), s32[]{:S(2)}) async-start(), calls=%async_computation | async-start | bytes 44040192 | tf_op jit(solution)/shard_map/psum | solution.py:77
  28.0 19.2 %copy-start.4 = (bf16[8192,1024]{1,0:T(8,128)(2,1)}, bf16[8192,1024]{1,0:T(8,128)(2,1)S(1)}, u32[]{:S(2)}) copy-start(bf16[8192,1024]{1,0:T(8,128)(2,1)S(1)} %get-tuple-element.12) | copy-start | bytes 50331652
  47.2 10.2 %copy-start.18 = (bf16[2,256,1024]{2,1,0:T(8,128)(2,1)S(1)}, bf16[2,256,1024]{2,1,0:T(8,128)(2,1)}, u32[]{:S(2)}) copy-start(bf16[2,256,1024]{2,1,0:T(8,128)(2,1)} %param.15) | copy-start | bytes 3145732
  53.4 2.0 copy-start.2
  67.8 23.1 %slice-start = ((s8[16777216]{0:T(1024)(128)(4,1)}), s8[4194304]{0:T(1024)(128)(4,1)S(1)}, s32[]{:S(2)}) async-start(s8[16777216]{0:T(1024)(128)(4,1)} %bitcast.79), calls=%async_computation.1 | async-start | bytes 8388608
  73.4 17.5 %slice-start.1 = ((s8[16777216]{0:T(1024)(128)(4,1)}), s8[4194304]{0:T(1024)(128)(4,1)S(1)}, s32[]{:S(2)}) async-start(s8[16777216]{0:T(1024)(128)(4,1)} %bitcast.79), calls=%async_computation.2 | async-start | bytes 8388608
  73.4 17.5 %slice-start.2 = ((s8[16777216]{0:T(1024)(128)(4,1)}), s8[4194304]{0:T(1024)(128)(4,1)S(1)}, s32[]{:S(2)}) async-start(s8[16777216]{0:T(1024)(128)(4,1)} %bitcast.79), calls=%async_computation.3 | async-start | bytes 8388608
  73.4 17.5 %slice-start.3 = ((s8[16777216]{0:T(1024)(128)(4,1)}), s8[4194304]{0:T(1024)(128)(4,1)S(1)}, s32[]{:S(2)}) async-start(s8[16777216]{0:T(1024)(128)(4,1)} %bitcast.79), calls=%async_computation.4 | async-start | bytes 8388608
  90.9 43.6 %copy-start.3 = (bf16[8192,256]{1,0:T(8,128)(2,1)S(1)}, bf16[8192,256]{1,0:T(8,128)(2,1)}, u32[]{:S(2)}) copy-start(bf16[8192,256]{1,0:T(8,128)(2,1)} %param.14) | copy-start | bytes 12582916
  90.9 43.6 %copy-start.19 = (bf16[2,1024,256]{2,1,0:T(8,128)(2,1)S(1)}, bf16[2,1024,256]{2,1,0:T(8,128)(2,1)}, u32[]{:S(2)}) copy-start(bf16[2,1024,256]{2,1,0:T(8,128)(2,1)} %param.16) | copy-start | bytes 3145732
  209.1 9.7 %copy-start.20 = (bf16[2,1024,256]{2,1,0:T(8,128)(2,1)S(1)}, bf16[2,1024,256]{2,1,0:T(8,128)(2,1)}, u32[]{:S(2)}) copy-start(bf16[2,1024,256]{2,1,0:T(8,128)(2,1)} %param.16) | copy-start | bytes 3145732
  218.8 28.4 %copy-start.1 = (bf16[8192,256]{1,0:T(8,128)(2,1)S(1)}, bf16[8192,256]{1,0:T(8,128)(2,1)}, u32[]{:S(2)}) copy-start(bf16[8192,256]{1,0:T(8,128)(2,1)} %param.13) | copy-start | bytes 12582916
  247.3 10.5 %copy-start.5 = (bf16[8192,1024]{1,0:T(8,128)(2,1)S(1)}, bf16[8192,1024]{1,0:T(8,128)(2,1)}, u32[]{:S(2)}) copy-start(bf16[8192,1024]{1,0:T(8,128)(2,1)} %fusion.7) | copy-start | bytes 50331652
  257.8 19.4 %copy-start.9 = (f32[1,256,256]{2,1,0:T(8,128)S(1)}, f32[1,256,256]{2,1,0:T(8,128)}, u32[]{:S(2)}) copy-start(f32[1,256,256]{2,1,0:T(8,128)} %convolution_bitcast_fusion.11) | copy-start | bytes 786436
  257.8 19.4 %copy-start.11 = (f32[1,256,256]{2,1,0:T(8,128)S(1)}, f32[1,256,256]{2,1,0:T(8,128)}, u32[]{:S(2)}) copy-start(f32[1,256,256]{2,1,0:T(8,128)} %convolution_bitcast_fusion.10) | copy-start | bytes 786436
  277.2 10.2 %copy-start.10 = (f32[1,256,256]{2,1,0:T(8,128)S(1)}, f32[1,256,256]{2,1,0:T(8,128)}, u32[]{:S(2)}) copy-start(f32[1,256,256]{2,1,0:T(8,128)} %convolution_bitcast_fusion.8) | copy-start | bytes 786436
  277.2 11.0 %copy-start.12 = (f32[1,1024,256]{2,1,0:T(8,128)S(1)}, f32[1,1024,256]{2,1,0:T(8,128)}, u32[]{:S(2)}) copy-start(f32[1,1024,256]{2,1,0:T(8,128)} %convolution_bitcast_fusion.5) | copy-start | bytes 3145732
  277.2 12.5 %copy-start.6 = (f32[1,1024,1024]{2,1,0:T(8,128)S(1)}, f32[1,1024,1024]{2,1,0:T(8,128)}, u32[]{:S(2)}) copy-start(f32[1,1024,1024]{2,1,0:T(8,128)} %convolution_bitcast_fusion.2) | copy-start | bytes 12582916
  277.2 12.5 %copy-start.7 = (f32[1,1024,1024]{2,1,0:T(8,128)S(1)}, f32[1,1024,1024]{2,1,0:T(8,128)}, u32[]{:S(2)}) copy-start(f32[1,1024,1024]{2,1,0:T(8,128)} %convolution_bitcast_fusion.3) | copy-start | bytes 12582916
  295.6 382.2 %copy-start.13 = (f32[2,256,256]{2,1,0:T(8,128)S(1)}, f32[2,256,256]{2,1,0:T(8,128)}, u32[]{:S(2)}) copy-start(f32[2,256,256]{2,1,0:T(8,128)} %param.24) | copy-start | bytes 1572868
  654.0 14.6 %copy-start.8 = (f32[2,1024,256]{2,1,0:T(8,128)S(1)}, f32[2,1024,256]{2,1,0:T(8,128)}, u32[]{:S(2)}) copy-start(f32[2,1024,256]{2,1,0:T(8,128)} %get-tuple-element.7) | copy-start | bytes 6291460
  654.1 27.0 %copy-start.14 = (f32[2,256,256]{2,1,0:T(8,128)S(1)}, f32[2,256,256]{2,1,0:T(8,128)}, u32[]{:S(2)}) copy-start(f32[2,256,256]{2,1,0:T(8,128)} %param.20) | copy-start | bytes 1572868
  654.1 27.0 %copy-start.15 = (f32[2,256,256]{2,1,0:T(8,128)S(1)}, f32[2,256,256]{2,1,0:T(8,128)}, u32[]{:S(2)}) copy-start(f32[2,256,256]{2,1,0:T(8,128)} %param.17) | copy-start | bytes 1572868
  654.1 27.0 %copy-start.16 = (f32[2,256,256]{2,1,0:T(8,128)S(1)}, f32[2,256,256]{2,1,0:T(8,128)}, u32[]{:S(2)}) copy-start(f32[2,256,256]{2,1,0:T(8,128)} %get-tuple-element.8) | copy-start | bytes 1572868
  654.1 27.0 %copy-start.17 = (f32[2,256,256]{2,1,0:T(8,128)S(1)}, f32[2,256,256]{2,1,0:T(8,128)}, u32[]{:S(2)}) copy-start(f32[2,256,256]{2,1,0:T(8,128)} %get-tuple-element.11) | copy-start | bytes 1572868
Sparse Core Ops, SparseCore 0:
  295.7 358.2 all-reduce.2
where the time goes:
time: 717 us; the launch traced here: 708 us
  waiting for transfers between devices  358 us (50%)
  matrix products  293 us (41%)
  other arithmetic  38.2 us (5%)
  between operations  15.4 us (2%)
    psum x1, waiting for transfers between devices, local_step(): totals = [lax.psum(part, 'data') for part in local_parts]  358 us
    dot_general x12, matrix products, cross_sum(): jnp.einsum('ti,tj->ij', left, right, preferred_element_type=jnp.float32)  168 us
    dot_general x2, matrix products, forward_backward(): jnp.einsum('tj,ij->ti', grad_down, w_down[block_idx], preferred_element_t...  54.9 us
    dot_general x2, matrix products, forward_backward(): jnp.dot(layer_in, w_up[block_idx], preferred_element_type=jnp.float32)  25.7 us
    add x2, other arithmetic, update_outputs(): factor_decay * old_part + (1.0 - factor_decay) * new_part  19.9 us
    div x6, other arithmetic, stacked_sums(): jnp.stack([cross_sum(left, right) for left, right in zip(left_list, right...  18.3 us
  transfers between devices with their start and end apart: 1, of which 1 were waited for; matrix products, arithmetic and copies ran while one was open for 0% of the time, Pallas kernels for 0%

commit v1 on v0

v1 whole, which is shorter than its diff:
```python
import functools
import jax
import jax.numpy as jnp
from jax import lax
from jax.experimental import pallas as pl
from jax.experimental.pallas import tpu as pltpu
from jax.sharding import PartitionSpec as P

C0 = 0.7978845608028654
C1 = C0 * 0.044715
BK = 256
ROWS = 1024
SUB = 64
BLOCKS = 60
PIECE = 1024
PIECES = BLOCKS * BK // PIECE
RING = 6
SLOT_ROWS = 992
VMEM_LIMIT = 67043328
PAIRS = [(i, j) for i in range(4) for j in range(i, 4)]
GRAM_H0, GRAM_U0, GRAM_Q1 = 0, 10, 11
GRAM_H1, DOWN1 = 12, 22
GRAM_G1, UP1, GRAM_U1, GRAM_E1 = 26, 36, 40, 41
UP0, DOWN0, GRAM_G0 = 42, 46, 50
STAGES = 8


def dot(left, right):
    return jnp.dot(left, right, preferred_element_type=jnp.float32)


def dot_nt(left, right):
    return lax.dot_general(left, right, (((1,), (1,)), ((), ())), preferred_element_type=jnp.float32)


def blk(index):
    return pl.ds(index * BK, BK)


class Exchange:
    def __init__(self, acc, slots, send, recv, free):
        self.acc, self.slots, self.send, self.recv, self.free = acc, slots, send, recv, free
        me = lax.axis_index("data")
        self.me = me
        self.core = lax.rem(me, 2)
        self.plane = (lax.rem(me // 2, 2), lax.rem(me // 4, 2))
        self.z = me // 8
        flip = lambda bit, step: me + (1 - 2 * bit) * step
        self.core_peer = flip(self.core, 1)
        self.plane_peer = (flip(self.plane[0], 2), flip(self.plane[1], 4))
        base = lax.rem(me, 8)
        self.z_peer = [base + 8 * lax.rem(self.z + d, 4) for d in (1, 2, 3)]

    def barrier(self):
        sem = pltpu.get_barrier_semaphore()
        peers = [self.core_peer, *self.plane_peer, *self.z_peer]
        for peer in peers:
            pl.semaphore_signal(sem, inc=1, device_id=(peer,), device_id_type=pl.DeviceIdType.MESH)
        pl.semaphore_wait(sem, len(peers))

    def rows(self, start, size):
        return self.acc.at[pl.ds(pl.multiple_of(start, 16), size), :]

    def spots(self, piece, color):
        first, second = (0, 1) if color == 0 else (1, 0)
        base1 = piece * PIECE + self.core * 512 + color * 256
        bit1, bit2 = self.plane[first], self.plane[second]
        base2 = base1 + bit1 * 128
        base3 = base2 + bit2 * 64
        return first, second, bit1, bit2, base1, base2, base3

    def copies(self, piece, stage):
        ring = piece % RING
        slot = self.slots.at[ring]
        found = []

        def add(number, src, dst, peer, keep=None, got=None):
            sem = stage * 6 + number
            found.append((pltpu.make_async_remote_copy(
                src_ref=src, dst_ref=dst, send_sem=self.send.at[ring, sem], recv_sem=self.recv.at[ring, sem],
                device_id=(peer,), device_id_type=pl.DeviceIdType.MESH), keep, got, peer))

        top = piece * PIECE
        if stage == 0:
            got = slot.at[pl.ds(0, 512), :]
            add(0, self.rows(top + (1 - self.core) * 512, 512), got, self.core_peer,
                (top + self.core * 512, 512), got)
        elif stage == 7:
            mine = self.rows(top + self.core * 512, 512)
            add(0, mine, mine, self.core_peer)
        for color in range(2):
            first, second, bit1, bit2, base1, base2, base3 = self.spots(piece, color)
            if stage == 1:
                got = slot.at[pl.ds(512 + color * 128, 128), :]
                add(color, self.rows(base1 + (1 - bit1) * 128, 128), got, self.plane_peer[first], (base2, 128), got)
            elif stage == 2:
                got = slot.at[pl.ds(768 + color * 64, 64), :]
                add(color, self.rows(base2 + (1 - bit2) * 64, 64), got, self.plane_peer[second], (base3, 64), got)
            elif stage == 3:
                for d in range(3):
                    got = slot.at[pl.ds(896 + color * 48 + d * 16, 16), :]
                    peer_z = lax.rem(self.z + d + 1, 4)
                    add(color * 3 + d, self.rows(base3 + peer_z * 16, 16), got, self.z_peer[d],
                        (base3 + self.z * 16, 16), got)
            elif stage == 4:
                mine = self.rows(base3 + self.z * 16, 16)
                for d in range(3):
                    add(color * 3 + d, mine, mine, self.z_peer[d])
            elif stage == 5:
                mine = self.rows(base3, 64)
                add(color, mine, mine, self.plane_peer[second])
            elif stage == 6:
                mine = self.rows(base2, 128)
                add(color, mine, mine, self.plane_peer[first])
        return found

    def credits(self, piece, stage):
        colors = 1 if stage == 0 else 2
        return [self.free.at[piece % RING, 2 * stage + color] for color in range(colors)]

    def start(self, piece, stage):
        found = self.copies(piece, stage)
        if stage >= STAGES // 2:
            credits = self.credits(piece, STAGES - 1 - stage)
            for credit in credits:
                pl.semaphore_wait(credit, len(found) // len(credits))
        for copy, *_ in found:
            copy.start()

    def finish(self, piece, stage):
        found = self.copies(piece, stage)
        for copy, *_ in found:
            copy.wait()
        if stage < STAGES // 2:
            credits = self.credits(piece, stage)
            per = len(found) // len(credits)
            for number, (_, _, _, peer) in enumerate(found):
                pl.semaphore_signal(credits[number // per], inc=1, device_id=(peer,),
                                    device_id_type=pl.DeviceIdType.MESH)
            for _, keep, got, _ in found:
                self.rows(*keep)[...] += got[...]

    def slot_of_time(self, events):
        for piece, stage in events:
            if stage > 0:
                self.finish(piece, stage - 1)
        for piece, stage in events:
            if stage < STAGES:
                self.start(piece, stage)


def cdf_of(pre):
    square = pre * pre
    return square, 0.5 * jnp.tanh(pre * (C1 * square + C0)) + 0.5


def slope_of(pre, square, cdf):
    return cdf * (((1.0 - cdf) * pre) * (6.0 * C1 * square + 2.0 * C0) + 1.0)


def produce_forward(col, u, w_ref, z_ref, h_ref):
    z_ref[...] = dot(u[...], w_ref[:, blk(col)]).astype(jnp.bfloat16)
    for row in range(0, ROWS, SUB):
        pre = z_ref[row:row + SUB, :].astype(jnp.float32)
        _, cdf = cdf_of(pre)
        h_ref[row:row + SUB, blk(col)] = (pre * cdf).astype(jnp.bfloat16)


def produce_both(col, u, w_ref, q, wd_ref, z_ref, d_ref, h_ref, g, off):
    z_ref[...] = dot(u[...], w_ref[:, blk(col)]).astype(jnp.bfloat16)
    d_ref[...] = dot_nt(q[...], wd_ref[blk(col), :]).astype(jnp.bfloat16)
    for row in range(0, ROWS, SUB):
        pre = z_ref[row:row + SUB, :].astype(jnp.float32)
        d_hidden = d_ref[row:row + SUB, :].astype(jnp.float32)
        square, cdf = cdf_of(pre)
        h_ref[row:row + SUB, blk(col)] = (pre * cdf).astype(jnp.bfloat16)
        g[pl.ds(off + row, SUB), blk(col)] = (d_hidden * slope_of(pre, square, cdf)).astype(jnp.bfloat16)


def kernel(tok_hbm, grad_hbm, w_up_hbm, w_down_hbm, out_hbm,
           acc, slots, tok, grad, mid, g1, w_up, w_down, z0, z1, d0, d1, h_ref, t_ref, ht_ref, small,
           send, recv, free, tok_sem, grad_sem, w_sem, out_sem):
    tiles = tok.shape[0] // ROWS
    w_copies = [pltpu.make_async_copy(w_up_hbm, w_up, w_sem.at[0]),
                pltpu.make_async_copy(w_down_hbm, w_down, w_sem.at[1])]

    def tile_copies(i):
        rows = pl.ds(pl.multiple_of(i * ROWS, ROWS), ROWS)
        return (pltpu.make_async_copy(tok_hbm.at[rows, :], tok.at[rows, :], tok_sem.at[i]),
                pltpu.make_async_copy(grad_hbm.at[rows, :], grad.at[rows, :], grad_sem.at[i]))

    for copy in w_copies:
        copy.start()
    for i in range(tiles):
        for copy in tile_copies(i):
            copy.start()
    exchange = Exchange(acc, slots, send, recv, free)
    exchange.barrier()

    @pl.loop(0, BLOCKS)
    def _(n):
        acc[pl.ds(pl.multiple_of(n * BK, BK), BK), :] = jnp.zeros((BK, BK), jnp.float32)

    for copy in w_copies:
        copy.wait()
    zs, ds_ = (z0, z1), (d0, d1)

    def out_copy(piece):
        rows = pl.ds(piece * PIECE, PIECE)
        return pltpu.make_async_copy(acc.at[rows, :], out_hbm.at[rows, :], out_sem.at[piece])

    starts = {}

    def events_at(now):
        return [(piece, now - first) for piece, first in starts.items() if 0 <= now - first <= STAGES]

    def fire(events):
        if events:
            exchange.slot_of_time(events)
            for piece, stage in events:
                if stage == STAGES:
                    out_copy(piece).start()

    def hooks(i, first):
        for n in range(tiles):
            events = events_at(first + n)
            if events:
                pl.when(i == n)(functools.partial(fire, events))

    def add_to(slot, value):
        acc[blk(slot), :] += value

    def gram_column(first, col, x):
        for i in range(col + 1):
            add_to(first + PAIRS.index((i, col)), dot(t_ref[blk(i), :], x(col)))

    def views(i):
        off = pl.multiple_of(i * ROWS, ROWS)
        rows = pl.ds(off, ROWS)
        return off, tok.at[rows, :], grad.at[rows, :], mid.at[rows, :]

    @pl.loop(0, tiles)
    def _(i):
        off, u, q, nxt = views(i)
        for copy in tile_copies(i):
            copy.wait()
        hx = lambda col: h_ref[:, blk(col)]

        def produce(col):
            produce_forward(col, u, w_up.at[0], zs[col % 2], h_ref)
            t_ref[blk(col), :] = h_ref[:, blk(col)].T

        produce(0)
        small[...] = u[...].T
        add_to(GRAM_U0, dot(small[...], u[...]))
        produce(1)
        gram_column(GRAM_H0, 0, hx)
        small[...] = q[...].T
        add_to(GRAM_Q1, dot(small[...], q[...]))
        produce(2)
        gram_column(GRAM_H0, 1, hx)
        produce(3)
        gram_column(GRAM_H0, 2, hx)
        nxt[...] = dot(h_ref[...], w_down[0]).astype(jnp.bfloat16)
        gram_column(GRAM_H0, 3, hx)

    starts.update({0: 8, 1: 9, 2: 10})

    @pl.loop(0, tiles)
    def _(i):
        hooks(i, 8)
        off, _, q, u = views(i)
        hx = lambda col: h_ref[:, blk(col)]

        def produce(col):
            produce_both(col, u, w_up.at[1], q, w_down.at[1], zs[col % 2], ds_[col % 2], h_ref, g1, off)
            t_ref[blk(col), :] = h_ref[:, blk(col)].T

        def consume(col):
            gram_column(GRAM_H1, col, hx)
            add_to(DOWN1 + col, dot(t_ref[blk(col), :], q[...]))

        produce(0)
        for col in range(1, 4):
            produce(col)
            consume(col - 1)
        consume(3)

    starts.update({3: 16, 4: 17, 5: 18})

    @pl.loop(0, tiles)
    def _(i):
        hooks(i, 16)
        off, _, _, u = views(i)
        rows = pl.ds(off, ROWS)
        gx = lambda col: g1[rows, blk(col)]
        small[...] = u[...].T
        add_to(GRAM_U1, dot(small[...], u[...]))
        for col in range(4):
            t_ref[blk(col), :] = gx(col).T
            add_to(UP1 + col, dot(small[...], gx(col)))
            gram_column(GRAM_G1, col, gx)
        u[...] = dot_nt(g1[rows, :], w_up[1]).astype(jnp.bfloat16)
        small[...] = u[...].T
        add_to(GRAM_E1, dot(small[...], u[...]))

    starts.update({6: 24, 7: 25, 8: 26, 9: 27})

    @pl.loop(0, tiles)
    def _(i):
        hooks(i, 24)
        off, u, _, q = views(i)
        rows = pl.ds(off, ROWS)

        def produce(col):
            produce_both(col, u, w_up.at[0], q, w_down.at[0], zs[col % 2], ds_[col % 2], h_ref, g1, off)
            ht_ref[blk(col % 2), :] = h_ref[:, blk(col)].T

        def consume(col):
            add_to(UP0 + col, dot(small[...], g1[rows, blk(col)]))
            add_to(DOWN0 + col, dot(ht_ref[blk(col % 2), :], q[...]))

        small[...] = u[...].T
        produce(0)
        for col in range(1, 4):
            produce(col)
            consume(col - 1)
        consume(3)

    starts.update({10: 32, 11: 33})

    def gram_row(row, now):
        halves = 2 if row < 2 else 1
        per = tiles // halves
        for half in range(halves):
            fire(events_at(now + half))

            @pl.loop(half * per, (half + 1) * per)
            def _(i):
                rows = pl.ds(pl.multiple_of(i * ROWS, ROWS), ROWS)
                small[...] = g1[rows, blk(row)].T
                for col in range(row, 4):
                    add_to(GRAM_G0 + PAIRS.index((row, col)), dot(small[...], g1[rows, blk(col)]))
        return now + halves

    now = gram_row(0, 32)
    starts[12] = max(now, 34)
    now = gram_row(1, now)
    starts[13] = now
    now = gram_row(2, now)
    now = gram_row(3, now)
    starts[14] = now
    while now <= max(starts.values()) + STAGES:
        fire(events_at(now))
        now += 1
    for piece in range(PIECES):
        out_copy(piece).wait()


def statistics(tok, grad, w_up, w_down):
    rows = tok.shape[0]
    tiles = rows // ROWS
    bf = lambda *shape: pltpu.VMEM(shape, jnp.bfloat16)
    any_spec = pl.BlockSpec(memory_space=pl.ANY)
    dma = pltpu.SemaphoreType.DMA
    return pl.pallas_call(
        kernel, name="statistics", in_specs=[any_spec] * 4, out_specs=any_spec,
        out_shape=jax.ShapeDtypeStruct((BLOCKS * BK, BK), jnp.float32),
        scratch_shapes=[
            pltpu.VMEM((BLOCKS * BK, BK), jnp.float32), pltpu.VMEM((RING, SLOT_ROWS, BK), jnp.float32),
            bf(rows, BK), bf(rows, BK), bf(rows, BK), bf(rows, 4 * BK), bf(*w_up.shape), bf(*w_down.shape),
            bf(ROWS, BK), bf(ROWS, BK), bf(ROWS, BK), bf(ROWS, BK),
            bf(ROWS, 4 * BK), bf(4 * BK, ROWS), bf(2 * BK, ROWS), bf(BK, ROWS),
            dma((RING, 6 * STAGES)), dma((RING, 6 * STAGES)),
            pltpu.SemaphoreType.REGULAR((RING, STAGES)), dma((tiles,)), dma((tiles,)), dma((2,)), dma((PIECES,))],
        cost_estimate=pl.CostEstimate(flops=100 * 10 ** 9, bytes_accessed=30 << 20, transcendentals=0),
        compiler_params=pltpu.CompilerParams(vmem_limit_bytes=VMEM_LIMIT, collective_id=0, has_side_effects=True),
    )(tok, grad, w_up, w_down)


def full_gram(packed, first):
    take = lambda n: packed[(first + n) * BK:(first + n + 1) * BK]
    pick = lambda i, j: take(PAIRS.index((i, j))) if i <= j else take(PAIRS.index((j, i))).T
    return jnp.concatenate([jnp.concatenate([pick(i, j) for j in range(4)], axis=1) for i in range(4)], axis=0)


def solution(mesh):
    axis_size = mesh.shape["data"]
    high = lax.Precision.HIGHEST

    def precise(left, right):
        return jnp.dot(left, right, precision=high, preferred_element_type=jnp.float32)

    def local_step(tok, grad, w_up, w_down, a_up_old, s_up_old, a_down_old, s_down_old,
                   a_up_inv, s_up_inv, a_down_inv, s_down_inv, factor_decay):
        packed = statistics(tok, grad, w_up, w_down)
        scale = 1.0 / (tok.shape[0] * axis_size)
        block = lambda n: packed[n * BK:(n + 1) * BK]
        across = lambda n: jnp.concatenate([block(n + i) for i in range(4)], axis=1)
        down = lambda n: packed[n * BK:(n + 4) * BK]
        keep, fresh = factor_decay, (1.0 - factor_decay) * scale
        stack = lambda first, second: jnp.stack([first, second])
        chain = lambda left, mid, right: precise(precise(left, mid * scale), right)
        return (stack(chain(a_up_inv[0], across(UP0), s_up_inv[0]), chain(a_up_inv[1], across(UP1), s_up_inv[1])),
                stack(chain(a_down_inv[0], down(DOWN0), s_down_inv[0]), chain(a_down_inv[1], down(DOWN1), s_down_inv[1])),
                keep * a_up_old + fresh * stack(block(GRAM_U0), block(GRAM_U1)),
                keep * s_up_old + fresh * stack(full_gram(packed, GRAM_G0), full_gram(packed, GRAM_G1)),
                keep * a_down_old + fresh * stack(full_gram(packed, GRAM_H0), full_gram(packed, GRAM_H1)),
                keep * s_down_old + fresh * stack(block(GRAM_E1), block(GRAM_Q1)))

    batch_spec = P("data", None)
    replicated = P()
    return jax.shard_map(local_step, mesh=mesh, in_specs=(batch_spec, batch_spec) + (replicated,) * 11,
                         out_specs=(replicated,) * 6, check_vma=False)
```

time: 717 us -> 406 us (0.57)
  waiting for transfers between devices: 358 us -> 0 us
  Pallas kernels: 0 us -> 264 us
  matrix products: 293 us -> 33.9 us
  local copies, waits for them, and re-layouts: 4.35 us -> 52.6 us
  between operations: 15.4 us -> 1.98 us
  other arithmetic: 38.2 us -> 46.3 us
    psum x1 -> x0, waiting for transfers between devices: 358 us -> none  [local_step(): totals = [lax.psum(part, 'data') for part in local_parts]]
    pallas_call x0 -> x1, Pallas kernels: none -> 264 us  [statistics(): pl.pallas_call(kernel, name='statistics', in_specs=[any_spec] * 4, out_sp...]
    dot_general x22 -> x8, matrix products: 293 us -> 33.9 us  [precise(): jnp.dot(left, right, precision=high, preferred_element_type=jnp.float32)]
    another operation x0 -> x6, other arithmetic: none -> 23.9 us  [local_step(): stack = lambda first, second: jnp.stack([first, second])]
    unnamed x50 -> x83, local copies, waits for them, and re-layouts: 4.35 us -> 27.5 us
    div x6 -> x0, other arithmetic: 18.3 us -> none  [stacked_sums(): jnp.stack([cross_sum(left, right) for left, right in zip(left_list, right...]
    another operation x0 -> x2, local copies, waits for them, and re-layouts: none -> 8.69 us  [local_step(): stack = lambda first, second: jnp.stack([first, second])]
  transfers between devices with their start and end apart: 1 -> 0, of which waited for: 1 -> 0; matrix products, arithmetic and copies ran while one was open for 0% -> 0% of each run, Pallas kernels for 0% -> 0%
where the time goes in v1:
time: 406 us; the launch traced here: 398 us
  Pallas kernels  264 us (65%)
  local copies, waits for them, and re-layouts  52.6 us (13%)
  other arithmetic  46.3 us (11%)
  matrix products  33.9 us (8%)
    pallas_call x1, Pallas kernels, statistics(): pl.pallas_call(kernel, name='statistics', in_specs=[any_spec] * 4, out_sp...  264 us
    dot_general x8, matrix products, precise(): jnp.dot(left, right, precision=high, preferred_element_type=jnp.float32)  33.9 us
    unnamed x83, local copies, waits for them, and re-layouts  27.5 us
    another operation x6, other arithmetic, local_step(): stack = lambda first, second: jnp.stack([first, second])  23.9 us
    add x1, other arithmetic, local_step(): keep * s_up_old  16.5 us
    another operation x2, local copies, waits for them, and re-layouts, local_step(): stack = lambda first, second: jnp.stack([first, second])  8.69 us

profile of v1, /device:TPU:0, one launch (start us, length us, event | category | flops | bytes accessed | tf_op | source)
XLA Modules:
  0.0 398.3 jit_solution(5411471648193108606)
XLA Ops:
  1.3 263.6 %statistics.1 = f32[15360,256]{1,0:T(8,128)} custom-call(bf16[8192,256]{1,0:T(8,128)(2,1)} %tok_hbm.1, bf16[8192,256]{1,0:T(8,128)(2,1)} %grad_hbm.1, bf16[2,256,1024]{2,1,0:T(8,128)(2,1)} %w_up_hbm.1, bf16[2,1024,256]{2,1,0:T(8,128)(2,1)} %w_down_hbm.1), custom_call_target="tpu_custom_call" | custom-call | flops 99999997952 | bytes 31457280 | tf_op jit(solution)/shard_map/statistics/pallas_call | solution.py:366
  264.9 9.3 %fusion.2 = f32[256,1024]{1,0:T(8,128)S(1)} fusion(f32[2,1024,1024]{2,1,0:T(8,128)} %param.23, f32[15360,256]{1,0:T(8,128)} %statistics.1), kind=kOutput, calls=%fused_computation.8 | convolution fusion | flops 3221487616 | bytes 6291456 | tf_op jit(solution)/shard_map/dot_general | solution.py:392
  274.2 2.9 convolution_bitcast_fusion
  277.1 8.3 %fusion.4 = f32[256,1024]{1,0:T(8,128)S(1)} fusion(f32[2,1024,1024]{2,1,0:T(8,128)S(1)} %copy-done.1, f32[15360,256]{1,0:T(8,128)} %statistics.1), kind=kOutput, calls=%fused_computation.10 | convolution fusion | flops 3221487616 | bytes 6291456 | tf_op jit(solution)/shard_map/dot_general | solution.py:392
  285.4 1.9 convolution_bitcast_fusion.1
  287.3 1.5 pad_maximum_fusion.1
  288.7 1.8 fusion.59
  290.5 2.2 fusion.20
  292.8 1.8 fusion.27
  294.6 3.7 fusion.17
  298.4 3.7 fusion.14
  302.1 1.5 pad_maximum_fusion
  303.6 4.4 %fusion.58 = (f32[256,256]{1,0:T(8,128)}, f32[256,256]{1,0:T(8,128)}, f32[256,256]{1,0:T(8,128)}, f32[256,256]{1,0:T(8,128)}, f32[256,256]{1,0:T(8,128)}, /*inde...) fusion(f32[15360,256]{1,0:T(8,128)} %statistics.1), kind=kLoop, calls=%fused_computation.92 | loop fusion | bytes 9961472 | tf_op jit(solution)/shard_map/slice | solution.py:382
  308.1 4.0 %slice_bitcast_fusion.1 = (f32[1,256,256]{2,1,0:T(8,128)S(1)}, f32[256,256]{0,1:T(8,128)}, f32[256,256]{0,1:T(8,128)}, f32[256,256]{0,1:T(8,128)}, f32[256,256]{...) fusion(f32[15360,256]{1,0:T(8,128)} %statistics.1), kind=kLoop, calls=%fused_computation.66 | loop fusion | bytes 9961472 | tf_op jit(solution)/shard_map/stack | solution.py:402
  312.2 4.6 %slice_bitcast_fusion = (f32[1,256,256]{2,1,0:T(8,128)S(1)}, f32[256,256]{1,0:T(8,128)}, f32[256,256]{1,0:T(8,128)}, f32[256,256]{1,0:T(8,128)}, f32[256,256]{1,...) fusion(f32[15360,256]{1,0:T(8,128)} %statistics.1), kind=kLoop, calls=%fused_computation.65 | loop fusion | bytes 9961472 | tf_op jit(solution)/shard_map/stack | solution.py:402
  320.8 1.9 copy.69
  323.8 1.9 copy.65
  325.7 1.8 copy.63
  327.4 1.8 copy.61
  338.4 1.8 copy.70
  340.2 1.8 copy.68
  343.5 1.8 copy.64
  345.3 1.8 copy.62
  347.0 1.8 copy.60
  351.4 1.8 copy.58
  353.2 1.8 copy.56
  357.6 5.0 %maximum_bitcast_fusion = f32[1,1024,1024]{2,1,0:T(8,128)} fusion(f32[256,256]{1,0:T(8,128)} %get-tuple-element.53, f32[256,256]{1,0:T(8,128)} %bitcast.106, f32[256,256]{1,0:T(8,128)} %copy.26, f32[256,256]{1,0:T(8,128)} %bitcast.107, f32[256,1024]{1,0:T(8,128)} %copy.28, f32[256,256]{1,0:T(8,128)} %get-tuple-element.56, f32[256,256]{1,0:T(8,128)} %get-tuple-element.57, ...), kind=kLoop, calls=%fused_computation.4 | loop fusion | flops 9437184 | bytes 8388608 | tf_op jit(solution)/shard_map/stack | solution.py:402
  362.6 1.3 copy.37
  364.0 4.8 %maximum_bitcast_fusion.1 = f32[1,1024,1024]{2,1,0:T(8,128)} fusion(f32[256,256]{1,0:T(8,128)} %get-tuple-element.43, f32[256,256]{1,0:T(8,128)} %bitcast.103, f32[256,256]{1,0:T(8,128)} %copy.36, f32[256,256]{1,0:T(8,128)} %bitcast.104, f32[256,1024]{1,0:T(8,128)S(1)} %copy.38, f32[256,256]{1,0:T(8,128)} %get-tuple-element.47, ...), kind=kLoop, calls=%fused_computation.5 | loop fusion | flops 9437184 | bytes 8388608 | tf_op jit(solution)/shard_map/stack | solution.py:402
  369.3 4.7 %maximum_bitcast_fusion.2 = f32[1,1024,1024]{2,1,0:T(8,128)} fusion(f32[256,256]{1,0:T(8,128)} %get-tuple-element.41, f32[256,256]{1,0:T(8,128)} %bitcast.100, f32[256,256]{1,0:T(8,128)} %copy.46, f32[256,256]{1,0:T(8,128)} %bitcast.101, f32[256,1024]{1,0:T(8,128)S(1)} %copy.48, f32[256,256]{1,0:T(8,128)} %get-tuple-element.51, ...), kind=kLoop, calls=%fused_computation.6 | loop fusion | flops 9437184 | bytes 8388608 | tf_op jit(solution)/shard_map/stack | solution.py:402
  375.2 6.5 %maximum_bitcast_fusion.3 = f32[1,1024,1024]{2,1,0:T(8,128)} fusion(f32[256,256]{1,0:T(8,128)} %get-tuple-element.59, f32[256,256]{1,0:T(8,128)} %copy.54, f32[256,256]{1,0:T(8,128)S(1)} %bitcast.98, f32[256,256]{1,0:T(8,128)} %copy.53, f32[256,256]{1,0:T(8,128)} %get-tuple-element.55, f32[256,256]{1,0:T(8,128)} %get-tuple-element.54, ...), kind=kLoop, calls=%fused_computation.7 | loop fusion | flops 12582912 | bytes 8388608 | tf_op jit(solution)/shard_map/stack | solution.py:402
  381.7 16.5 %fusion = (f32[2,1024,1024]{2,1,0:T(8,128)}, f32[2,1024,1024]{2,1,0:T(8,128)}) fusion(f32[1,1024,1024]{2,1,0:T(8,128)} %maximum_bitcast_fusion.1, f32[1,1024,1024]{2,1,0:T(8,128)S(1)} %copy-done, f32[2,1024,1024]{2,1,0:T(8,128)} %param.18, f32[]{:T(128)S(6)} %mul.61, f32[]{:T(128)S(6)} %copy.80, f32[1,1024,1024]{2,1,0:T(8,128)} %maximum_bitcast_fusion.3, ...), kind=kLoop, calls=%fused_computation.1 | loop fusion | flops 16777216 | bytes 50331656 | tf_op jit(solution)/shard_map/add | solution.py:407
  (93 shorter events, 22.5 us)
Async XLA Ops:
  264.9 12.2 %copy-start.1 = (f32[2,1024,1024]{2,1,0:T(8,128)S(1)}, f32[2,1024,1024]{2,1,0:T(8,128)}, u32[]{:S(2)}) copy-start(f32[2,1024,1024]{2,1,0:T(8,128)} %param.23) | copy-start | bytes 25165828
  274.2 11.2 %copy-start.25 = (f32[2,256,256]{2,1,0:T(8,128)S(1)}, f32[2,256,256]{2,1,0:T(8,128)}, u32[]{:S(2)}) copy-start(f32[2,256,256]{2,1,0:T(8,128)} %param.24) | copy-start | bytes 1572868
  285.4 9.2 %slice-start = ((s8[8388608]{0:T(1024)(128)(4,1)}), s8[4194304]{0:T(1024)(128)(4,1)S(1)}, s32[]{:S(2)}) async-start(s8[8388608]{0:T(1024)(128)(4,1)} %bitcast.96), calls=%async_computation | async-start | bytes 8388608
  287.3 3.3 copy-start.26
  288.7 5.9 %slice-start.1 = ((s8[8388608]{0:T(1024)(128)(4,1)}), s8[4194304]{0:T(1024)(128)(4,1)S(1)}, s32[]{:S(2)}) async-start(s8[8388608]{0:T(1024)(128)(4,1)} %bitcast.96), calls=%async_computation.1 | async-start | bytes 8388608
  312.2 4.7 %copy-start.27 = (f32[2,256,256]{2,1,0:T(8,128)S(1)}, f32[2,256,256]{2,1,0:T(8,128)}, u32[]{:S(2)}) copy-start(f32[2,256,256]{2,1,0:T(8,128)} %param.17) | copy-start | bytes 1572868
  312.2 4.7 %copy-start.28 = (f32[2,256,256]{2,1,0:T(8,128)S(1)}, f32[2,256,256]{2,1,0:T(8,128)}, u32[]{:S(2)}) copy-start(f32[2,256,256]{2,1,0:T(8,128)} %param.20) | copy-start | bytes 1572868
  318.0 11.3 %copy-start.17 = (f32[256,256]{1,0:T(8,128)S(1)}, f32[256,256]{1,0:T(8,128)}, u32[]{:S(2)}) copy-start(f32[256,256]{1,0:T(8,128)} %get-tuple-element.37) | copy-start | bytes 786436
  318.0 12.1 %copy-start.16 = (f32[256,256]{1,0:T(8,128)S(1)}, f32[256,256]{1,0:T(8,128)}, u32[]{:S(2)}) copy-start(f32[256,256]{1,0:T(8,128)} %get-tuple-element.39) | copy-start | bytes 786436
  318.0 12.9 %copy-start.14 = (f32[256,256]{0,1:T(8,128)S(1)}, f32[256,256]{0,1:T(8,128)}, u32[]{:S(2)}) copy-start(f32[256,256]{0,1:T(8,128)} %get-tuple-element.9) | copy-start | bytes 786436
  318.0 13.8 %copy-start.13 = (f32[256,256]{0,1:T(8,128)S(1)}, f32[256,256]{0,1:T(8,128)}, u32[]{:S(2)}) copy-start(f32[256,256]{0,1:T(8,128)} %get-tuple-element.12) | copy-start | bytes 786436
  319.9 17.0 %copy-start.4 = (f32[256,256]{0,1:T(8,128)}, f32[256,256]{0,1:T(8,128)S(1)}, u32[]{:S(2)}) copy-start(f32[256,256]{0,1:T(8,128)S(1)} %copy.73) | copy-start | bytes 786436
  323.8 18.3 %copy-start.7 = (f32[256,256]{0,1:T(8,128)}, f32[256,256]{0,1:T(8,128)S(1)}, u32[]{:S(2)}) copy-start(f32[256,256]{0,1:T(8,128)S(1)} %copy.67) | copy-start | bytes 786436
  333.4 8.5 %copy-start.15 = (f32[256,256]{1,0:T(8,128)S(1)}, f32[256,256]{1,0:T(8,128)}, u32[]{:S(2)}) copy-start(f32[256,256]{1,0:T(8,128)} %get-tuple-element.30) | copy-start | bytes 786436
  334.3 7.8 %copy-start.19 = (f32[256,256]{0,1:T(8,128)S(1)}, f32[256,256]{0,1:T(8,128)}, u32[]{:S(2)}) copy-start(f32[256,256]{0,1:T(8,128)} %get-tuple-element.10) | copy-start | bytes 786436
  357.6 5.0 %copy-start.8 = (f32[256,256]{0,1:T(8,128)S(1)}, f32[256,256]{0,1:T(8,128)}, u32[]{:S(2)}) copy-start(f32[256,256]{0,1:T(8,128)} %copy.65) | copy-start | bytes 786436
  357.6 5.0 %copy-start.9 = (f32[256,256]{0,1:T(8,128)S(1)}, f32[256,256]{0,1:T(8,128)}, u32[]{:S(2)}) copy-start(f32[256,256]{0,1:T(8,128)} %copy.63) | copy-start | bytes 786436
  357.6 5.0 %copy-start.23 = (f32[256,256]{0,1:T(8,128)S(1)}, f32[256,256]{0,1:T(8,128)}, u32[]{:S(2)}) copy-start(f32[256,256]{0,1:T(8,128)} %copy.64) | copy-start | bytes 786436
  357.6 5.0 %copy-start.24 = (f32[256,256]{0,1:T(8,128)S(1)}, f32[256,256]{0,1:T(8,128)}, u32[]{:S(2)}) copy-start(f32[256,256]{0,1:T(8,128)} %copy.62) | copy-start | bytes 786436
  363.9 4.8 %copy-start.5 = (f32[256,256]{0,1:T(8,128)S(1)}, f32[256,256]{0,1:T(8,128)}, u32[]{:S(2)}) copy-start(f32[256,256]{0,1:T(8,128)} %copy.71) | copy-start | bytes 786436
  363.9 4.8 %copy-start.6 = (f32[256,256]{0,1:T(8,128)S(1)}, f32[256,256]{0,1:T(8,128)}, u32[]{:S(2)}) copy-start(f32[256,256]{0,1:T(8,128)} %copy.69) | copy-start | bytes 786436
  363.9 4.9 %copy-start.21 = (f32[256,256]{0,1:T(8,128)S(1)}, f32[256,256]{0,1:T(8,128)}, u32[]{:S(2)}) copy-start(f32[256,256]{0,1:T(8,128)} %copy.70) | copy-start | bytes 786436
  364.0 4.9 %copy-start.22 = (f32[256,256]{0,1:T(8,128)S(1)}, f32[256,256]{0,1:T(8,128)}, u32[]{:S(2)}) copy-start(f32[256,256]{0,1:T(8,128)} %copy.68) | copy-start | bytes 786436
  369.2 4.7 %copy-start.2 = (f32[256,256]{0,1:T(8,128)S(1)}, f32[256,256]{0,1:T(8,128)}, u32[]{:S(2)}) copy-start(f32[256,256]{0,1:T(8,128)} %copy.75) | copy-start | bytes 786436
  369.3 4.7 %copy-start.18 = (f32[256,256]{0,1:T(8,128)S(1)}, f32[256,256]{0,1:T(8,128)}, u32[]{:S(2)}) copy-start(f32[256,256]{0,1:T(8,128)} %get-tuple-element.16) | copy-start | bytes 786436
  369.3 4.7 %copy-start.20 = (f32[256,256]{0,1:T(8,128)S(1)}, f32[256,256]{0,1:T(8,128)}, u32[]{:S(2)}) copy-start(f32[256,256]{0,1:T(8,128)} %copy.74) | copy-start | bytes 786436
  374.0 1.0 copy-start.3
  374.0 1.0 copy-start.10
  374.0 1.1 copy-start.11
  374.0 1.2 copy-start.12
  375.2 6.5 %copy-start = (f32[1,1024,1024]{2,1,0:T(8,128)S(1)}, f32[1,1024,1024]{2,1,0:T(8,128)}, u32[]{:S(2)}) copy-start(f32[1,1024,1024]{2,1,0:T(8,128)} %maximum_bitcast_fusion) | copy-start | bytes 12582916
